TPU v7x, 32 devices: a whole 2x2x4 slice. The times are simulated.
32 devices in a mesh: dp: 2 (over y), ep: 16 (over z, x, core).
Axes of the slice: x: 2, y: 2, z: 4, core: 2. Of those that a mesh axis runs over, the one named last changes fastest.
Arguments:
- tokens: bfloat16 [16, 2, 1, 3584], P('ep', 'dp'), may hold values from -6 to 6
- gate_weights: bfloat16 [16, 2, 1, 8], P('ep', 'dp'), may hold values from 0.099609375 to 0.59765625
- expert_ids: int32 [16, 2, 1, 8], P('ep', 'dp'), may hold values from 0 to 15, all different within a row; in each aligned block of 2 rows (0 to 1, 2 to 3, ..., all dimensions but the last counted through in order) at most 2 rows name the same one
- gate_proj: bfloat16 [16, 3584, 2048], P('ep', None, 'dp'), may hold values from -0.09375 to 0.09375
- up_proj: bfloat16 [16, 3584, 2048], P('ep', None, 'dp'), may hold values from -0.09375 to 0.09375
- down_proj: bfloat16 [16, 2048, 3584], P('ep', 'dp'), may hold values from -0.125 to 0.125
Outputs:
- mixed: bfloat16 [16, 2, 1, 3584], P('ep', 'dp')
Inputs may be any that keep to these rules, and one draw needn't show every extreme that they name: `expert_ids`: each token names 8 different experts. Among the 2 tokens of one index of the first dimension, no expert is named more than 2 times, a bound that some block reaches.
All inputs are finite; a program needn't handle non-finite values.
Results may differ from a plain program's by a relative error of at most 0.02.
Values may be sent and summed in bfloat16 or wider, within the bound.
A program may use at most 64 MiB of HBM per device.

v0:
```python
import jax
import jax.numpy as jnp
from jax import lax
from jax.sharding import PartitionSpec as P


def placing(flat_ids, expert_count, capacity):
    labels = jnp.arange(expert_count, dtype=jnp.int32)
    onehot = (flat_ids[:, None] == labels[None, :]).astype(jnp.int32)
    earlier = jnp.cumsum(onehot, axis=0) - onehot
    slot_index = jnp.sum(earlier * onehot, axis=1)
    destination = flat_ids * capacity + slot_index
    targets = jnp.arange(expert_count * capacity, dtype=jnp.int32)
    return (destination[:, None] == targets[None, :]).astype(jnp.float32)


def body(tokens, gate_weights, expert_ids, gate_proj, up_proj, down_proj):
    group_count = lax.axis_size("dp")
    expert_count = lax.axis_size("ep")
    token_count = tokens.shape[2]
    feature_count = tokens.shape[3]
    top_count = expert_ids.shape[3]
    capacity = min(
        group_count * token_count, token_count * (group_count * top_count // expert_count + 1)
    )
    token_total = group_count * token_count
    slot_total = expert_count * capacity
    column_count = feature_count // group_count
    all_ids = lax.all_gather(expert_ids, "dp", axis=1, tiled=True)
    placed = placing(all_ids.reshape(-1), expert_count, capacity)
    selection = jnp.sum(placed.reshape(token_total, top_count, slot_total), axis=1)
    selection_t = selection.T.astype(jnp.bfloat16)
    token_rows, all_weights = (
        lax.all_gather(tokens, "dp", axis=1, tiled=True),
        lax.all_gather(gate_weights, "dp", axis=1, tiled=True),
    )
    buffer = jnp.dot(
        selection_t,
        token_rows.reshape(token_total, feature_count),
        preferred_element_type=jnp.float32,
    ).astype(jnp.bfloat16)
    received = lax.all_to_all(
        buffer.reshape(expert_count, capacity, feature_count),
        "ep",
        split_axis=0,
        concat_axis=0,
        tiled=True,
    )
    slot_rows = received.reshape(slot_total, feature_count)
    gate_act = jnp.dot(slot_rows, gate_proj[0], preferred_element_type=jnp.float32)
    up_act = jnp.dot(slot_rows, up_proj[0], preferred_element_type=jnp.float32)
    hidden = (jax.nn.silu(gate_act) * up_act).astype(jnp.bfloat16)
    down_mat = down_proj[0]
    summed_t = lax.psum_scatter(
        lax.dot_general(
            down_mat, hidden, (((0,), (1,)), ((), ())), preferred_element_type=jnp.float32
        ).astype(jnp.bfloat16),
        "dp",
        scatter_dimension=0,
        tiled=True,
    ).astype(jnp.float32)
    summed = summed_t.T.astype(jnp.bfloat16).reshape(expert_count, capacity, column_count)
    returned = lax.all_to_all(summed, "ep", split_axis=0, concat_axis=0, tiled=True)
    weight_flat = all_weights.reshape(-1).astype(jnp.float32)
    weighted = jnp.sum(
        (placed * weight_flat[:, None]).reshape(token_total, top_count, slot_total), axis=1
    )
    mixed = jnp.dot(
        weighted,
        returned.reshape(slot_total, column_count).astype(jnp.float32),
        precision=lax.Precision.HIGHEST,
    ).astype(jnp.bfloat16)
    own = lax.all_to_all(
        mixed.reshape(group_count, token_count, column_count),
        "dp",
        split_axis=0,
        concat_axis=2,
        tiled=True,
    )
    return own.reshape(1, 1, token_count, feature_count)


def solution(mesh):
    placed = (
        P("ep", "dp", None, None),
        P("ep", "dp", None, None),
        P("ep", "dp", None, None),
        P("ep", None, "dp"),
        P("ep", None, "dp"),
        P("ep", "dp", None),
    )
    return jax.shard_map(
        body, mesh=mesh, in_specs=placed, out_specs=P("ep", "dp", None, None), check_vma=False
    )
```

profile of v0, /device:TPU:0, one launch (start us, length us, event | category | flops | bytes accessed | tf_op | source)
XLA Modules:
  0.0 90.4 jit_solution(14572636809706801968)
XLA Ops:
  6.5 0.0 reduce-scatter.2.cloned.1.call-start
  6.5 5.4 %all_gather.9 = s32[1,2,1,8]{3,2,0,1:T(1,128)S(1)} all-gather(s32[1,1,1,8]{3,2,0,1:T(1,128)} %bitcast.43), channel_id=1, replica_groups=mesh['dp'=2,'ep'=16] {'dp'}, dimensions={1}, use_global_device_ids=true | all-gather | bytes 96 | tf_op jit(solution)/shard_map/all_gather | solution.py:29
  11.9 0.5 broadcast.39
  12.4 0.7 fusion.32
  13.1 0.1 eq.30
  13.2 0.1 fusion.29
  13.3 0.2 select_reduce_fusion.1
  13.5 0.1 reduce_sum.30
  13.6 4.4 %all_gather.10 = bf16[1,2,1,8]{3,2,0,1:T(2,128)(2,1)S(1)} all-gather(bf16[1,1,1,8]{3,2,0,1:T(2,128)(2,1)} %bitcast.44), channel_id=1, replica_groups=mesh['dp'=2,'ep'=16] {'dp'}, dimensions={1}, use_global_device_ids=true | all-gather | bytes 48 | tf_op jit(solution)/shard_map/all_gather | solution.py:35
  17.9 4.6 %all_gather.11 = bf16[1,2,1,3584]{3,2,0,1:T(2,128)(2,1)S(1)} all-gather(bf16[1,1,1,3584]{3,2,0,1:T(2,128)(2,1)} %bitcast.40), channel_id=1, replica_groups=mesh['dp'=2,'ep'=16] {'dp'}, dimensions={1}, use_global_device_ids=true | all-gather | bytes 21504 | tf_op jit(solution)/shard_map/all_gather | solution.py:34
  22.6 0.1 convert_reduce_fusion
  22.6 0.3 convolution_convert_fusion
  22.9 0.1 reshape.70
  23.0 15.6 %all_to_all.19 = bf16[16,2,3584]{2,1,0:T(2,128)(2,1)S(1)} all-to-all(bf16[16,2,3584]{2,1,0:T(2,128)(2,1)S(1)} %reshape.70), channel_id=1, replica_groups=mesh['dp'=2,'ep'=16] {'ep'}, dimensions={0} | all-to-all | bytes 458752 | tf_op jit(solution)/shard_map/all_to_all | solution.py:42
  38.7 0.1 reshape.71
  38.7 4.4 %fusion.4 = f32[32,1024]{1,0:T(8,128)S(1)} fusion(bf16[32,3584]{1,0:T(8,128)(2,1)S(1)} %reshape.71, bf16[1,3584,1024]{2,1,0:T(8,128)(2,1)} %param.9), kind=kOutput, calls=%fused_computation.4 | convolution fusion | flops 234881024 | bytes 7700480 | tf_op jit(solution)/shard_map/dot_general | solution.py:50
  43.2 8.5 %fusion.9 = bf16[3584,32]{0,1:T(8,128)(2,1)} fusion(bf16[1,1024,3584]{2,1,0:T(8,128)(2,1)} %param.11, bf16[32,3584]{1,0:T(8,128)(2,1)S(1)} %reshape.71, bf16[1,3584,1024]{2,1,0:T(8,128)(2,1)} %param.10, f32[32,1024]{1,0:T(8,128)S(1)} %fusion.4), kind=kOutput, calls=%fused_computation.8 | convolution fusion | flops 470073344 | bytes 15269888 | tf_op jit(solution)/shard_map/dot_general | solution.py:55
  51.7 0.0 reduce-scatter.2.cloned.1.call-update
  51.7 9.6 %reduce-scatter.2.cloned.1.call-done = bf16[1792,32]{0,1:T(8,128)(2,1)} async-done(((bf16[3584,32]{0,1:T(8,128)(2,1)}), bf16[1792,32]{0,1:T(8,128)(2,1)}) %reduce-scatter.2.cloned.1.call-update) | async-done | bytes 114704 | tf_op jit(solution)/shard_map/reduce_scatter | solution.py:54
  61.3 0.9 %reshape.72 = bf16[16,2,1792]{2,1,0:T(2,128)(2,1)S(1)} reshape(bf16[32,1792]{1,0:T(8,128)(2,1)} %bitcast.39) | data formatting | bytes 229376 | tf_op jit(solution)/shard_map/reshape | solution.py:62
  62.3 13.0 %all_to_all.20 = bf16[16,2,1792]{2,1,0:T(2,128)(2,1)S(1)} all-to-all(bf16[16,2,1792]{2,1,0:T(2,128)(2,1)S(1)} %reshape.72), channel_id=1, replica_groups=mesh['dp'=2,'ep'=16] {'ep'}, dimensions={0} | all-to-all | bytes 229376 | tf_op jit(solution)/shard_map/all_to_all | solution.py:63
  75.4 0.2 fusion.12
  75.6 0.5 broadcast.40
  76.1 0.7 reduce.5
  76.8 6.1 %all_to_all.21 = bf16[2,2,896]{2,1,0:T(2,128)(2,1)S(1)} all-to-all(bf16[2,2,896]{2,1,0:T(2,128)(2,1)S(1)} %reshape.86), channel_id=1, replica_groups=mesh['dp'=2,'ep'=16] {'dp'}, dimensions={0} | all-to-all | bytes 14336 | tf_op jit(solution)/shard_map/all_to_all | solution.py:73
  82.9 0.6 reshape.87
  (5 shorter events, 0.1 us)
Async XLA Ops:
  6.5 54.8 %reduce-scatter.2.cloned.1.call-start = ((), (), s32[]{:S(2)}) async-start(), calls=%async_computation.4 | async-start | bytes 344064 | tf_op jit(solution)/shard_map/reduce_scatter | solution.py:54
Sparse Core Ops, SparseCore 0:
  51.8 9.4 reduce-scatter.1
where the time goes:
time: 90.7 us; the launch traced here: 90.4 us
  blocking collectives  49.2 us (54%)
  matrix products  13.4 us (15%)
  between operations  13.4 us (15%)
  waiting for transfers between devices  9.65 us (11%)
  local copies, waits for them, and re-layouts  3 us (3%)
  other arithmetic  1.72 us (2%)
    all_to_all x1, blocking collectives, body(): lax.all_to_all(buffer.reshape(expert_count, capacity, feature_count), 'ep...  15.6 us
    all_to_all x1, blocking collectives, body(): lax.all_to_all(summed, 'ep', split_axis=0, concat_axis=0, tiled=True)  13 us
    reduce_scatter x1, waiting for transfers between devices, body(): lax.psum_scatter(lax.dot_general(down_mat, hidden, (((0,), (1,)), ((), ()...  9.63 us
    dot_general x1, matrix products, body(): lax.dot_general(down_mat, hidden, (((0,), (1,)), ((), ())), preferred_ele...  8.5 us
    all_to_all x1, blocking collectives, body(): lax.all_to_all(mixed.reshape(group_count, token_count, column_count), 'dp...  6.14 us
    all_gather x1, blocking collectives, body(): all_ids = lax.all_gather(expert_ids, 'dp', axis=1, tiled=True)  5.38 us
    all_gather x1, blocking collectives, body(): lax.all_gather(tokens, 'dp', axis=1, tiled=True)  4.61 us
    dot_general x1, matrix products, body(): jnp.dot(slot_rows, gate_proj[0], preferred_element_type=jnp.float32)  4.45 us
  transfers between devices with their start and end apart: 1, of which 1 were waited for; matrix products, arithmetic and copies ran while one was open for 0% of the time, Pallas kernels for 0%

commit v1 on v0

--- a/solution.py
+++ b/solution.py
@@ -70,12 +70,20 @@
         returned.reshape(slot_total, column_count).astype(jnp.float32),
         precision=lax.Precision.HIGHEST,
     ).astype(jnp.bfloat16)
-    own = lax.all_to_all(
-        mixed.reshape(group_count, token_count, column_count),
-        "dp",
-        split_axis=0,
-        concat_axis=2,
-        tiled=True,
+    own = jnp.concatenate(
+        lax.all_to_all(
+            jnp.stack(
+                jnp.split(
+                    mixed.reshape(group_count, token_count, column_count),
+                    lax.axis_size("dp"),
+                    axis=0,
+                )
+            ),
+            "dp",
+            0,
+            0,
+        ),
+        axis=2,
     )
     return own.reshape(1, 1, token_count, feature_count)
 

time: 90.7 us -> 90.8 us (level)
  no operation moved by 1% of the time
where the time goes in v1:
time: 90.8 us; the launch traced here: 90.5 us
  blocking collectives  49.2 us (54%)
  matrix products  13.4 us (15%)
  between operations  13.4 us (15%)
  waiting for transfers between devices  9.65 us (11%)
  local copies, waits for them, and re-layouts  3.02 us (3%)
  other arithmetic  1.78 us (2%)
    all_to_all x1, blocking collectives, body(): lax.all_to_all(buffer.reshape(expert_count, capacity, feature_count), 'ep...  15.6 us
    all_to_all x1, blocking collectives, body(): lax.all_to_all(summed, 'ep', split_axis=0, concat_axis=0, tiled=True)  13 us
    reduce_scatter x1, waiting for transfers between devices, body(): lax.psum_scatter(lax.dot_general(down_mat, hidden, (((0,), (1,)), ((), ()...  9.63 us
    dot_general x1, matrix products, body(): lax.dot_general(down_mat, hidden, (((0,), (1,)), ((), ())), preferred_ele...  8.5 us
    all_to_all x1, blocking collectives, body(): lax.all_to_all(jnp.stack(jnp.split(mixed.reshape(group_count, token_count...  6.14 us
    all_gather x1, blocking collectives, body(): all_ids = lax.all_gather(expert_ids, 'dp', axis=1, tiled=True)  5.38 us
    all_gather x1, blocking collectives, body(): lax.all_gather(tokens, 'dp', axis=1, tiled=True)  4.61 us
    dot_general x1, matrix products, body(): jnp.dot(slot_rows, gate_proj[0], preferred_element_type=jnp.float32)  4.45 us
  transfers between devices with their start and end apart: 1, of which 1 were waited for; matrix products, arithmetic and copies ran while one was open for 0% of the time, Pallas kernels for 0%

profile of v1, /device:TPU:0, one launch (start us, length us, event | category | flops | bytes accessed | tf_op | source)
XLA Modules:
  0.0 90.5 jit_solution(18156122526975307088)
XLA Ops:
  6.5 0.0 reduce-scatter.2.cloned.1.call-start
  6.5 5.4 %all_gather.9 = s32[1,2,1,8]{3,2,0,1:T(1,128)S(1)} all-gather(s32[1,1,1,8]{3,2,0,1:T(1,128)} %bitcast.45), channel_id=1, replica_groups=mesh['dp'=2,'ep'=16] {'dp'}, dimensions={1}, use_global_device_ids=true | all-gather | bytes 96 | tf_op jit(solution)/shard_map/all_gather | solution.py:29
  11.9 0.5 broadcast.39
  12.4 0.7 fusion.31
  13.1 0.1 eq.30
  13.2 0.1 fusion.28
  13.3 0.2 select_reduce_fusion.1
  13.5 0.1 reduce_sum.30
  13.6 4.4 %all_gather.10 = bf16[1,2,1,8]{3,2,0,1:T(2,128)(2,1)S(1)} all-gather(bf16[1,1,1,8]{3,2,0,1:T(2,128)(2,1)} %bitcast.46), channel_id=1, replica_groups=mesh['dp'=2,'ep'=16] {'dp'}, dimensions={1}, use_global_device_ids=true | all-gather | bytes 48 | tf_op jit(solution)/shard_map/all_gather | solution.py:35
  17.9 4.6 %all_gather.11 = bf16[1,2,1,3584]{3,2,0,1:T(2,128)(2,1)S(1)} all-gather(bf16[1,1,1,3584]{3,2,0,1:T(2,128)(2,1)} %bitcast.42), channel_id=1, replica_groups=mesh['dp'=2,'ep'=16] {'dp'}, dimensions={1}, use_global_device_ids=true | all-gather | bytes 21504 | tf_op jit(solution)/shard_map/all_gather | solution.py:34
  22.6 0.1 convert_reduce_fusion
  22.6 0.3 convolution_convert_fusion
  22.9 0.1 reshape.65
  23.0 15.6 %all_to_all.15 = bf16[16,2,3584]{2,1,0:T(2,128)(2,1)S(1)} all-to-all(bf16[16,2,3584]{2,1,0:T(2,128)(2,1)S(1)} %reshape.65), channel_id=1, replica_groups=mesh['dp'=2,'ep'=16] {'ep'}, dimensions={0} | all-to-all | bytes 458752 | tf_op jit(solution)/shard_map/all_to_all | solution.py:42
  38.7 0.1 reshape.66
  38.7 4.4 %fusion.4 = f32[32,1024]{1,0:T(8,128)S(1)} fusion(bf16[32,3584]{1,0:T(8,128)(2,1)S(1)} %reshape.66, bf16[1,3584,1024]{2,1,0:T(8,128)(2,1)} %param.9), kind=kOutput, calls=%fused_computation.4 | convolution fusion | flops 234881024 | bytes 7700480 | tf_op jit(solution)/shard_map/dot_general | solution.py:50
  43.2 8.5 %fusion.9 = bf16[3584,32]{0,1:T(8,128)(2,1)} fusion(bf16[1,1024,3584]{2,1,0:T(8,128)(2,1)} %param.11, bf16[32,3584]{1,0:T(8,128)(2,1)S(1)} %reshape.66, bf16[1,3584,1024]{2,1,0:T(8,128)(2,1)} %param.10, f32[32,1024]{1,0:T(8,128)S(1)} %fusion.4), kind=kOutput, calls=%fused_computation.8 | convolution fusion | flops 470073344 | bytes 15269888 | tf_op jit(solution)/shard_map/dot_general | solution.py:55
  51.7 0.0 reduce-scatter.2.cloned.1.call-update
  51.7 9.6 %reduce-scatter.2.cloned.1.call-done = bf16[1792,32]{0,1:T(8,128)(2,1)} async-done(((bf16[3584,32]{0,1:T(8,128)(2,1)}), bf16[1792,32]{0,1:T(8,128)(2,1)}) %reduce-scatter.2.cloned.1.call-update) | async-done | bytes 114704 | tf_op jit(solution)/shard_map/reduce_scatter | solution.py:54
  61.3 0.9 %reshape.67 = bf16[16,2,1792]{2,1,0:T(2,128)(2,1)S(1)} reshape(bf16[32,1792]{1,0:T(8,128)(2,1)} %bitcast.41) | data formatting | bytes 229376 | tf_op jit(solution)/shard_map/reshape | solution.py:62
  62.3 13.0 %all_to_all.16 = bf16[16,2,1792]{2,1,0:T(2,128)(2,1)S(1)} all-to-all(bf16[16,2,1792]{2,1,0:T(2,128)(2,1)S(1)} %reshape.67), channel_id=1, replica_groups=mesh['dp'=2,'ep'=16] {'ep'}, dimensions={0} | all-to-all | bytes 229376 | tf_op jit(solution)/shard_map/all_to_all | solution.py:63
  75.4 0.2 convolution_convert_fusion.1
  75.6 0.5 broadcast.40
  76.1 0.7 reduce.5
  76.8 6.1 %all_to_all.17 = bf16[2,2,896]{2,1,0:T(2,128)(2,1)S(1)} all-to-all(bf16[2,2,896]{2,1,0:T(2,128)(2,1)S(1)} %reshape.79), channel_id=1, replica_groups=mesh['dp'=2,'ep'=16] {'dp'}, dimensions={0} | all-to-all | bytes 14336 | tf_op jit(solution)/shard_map/all_to_all | solution.py:74
  83.0 0.6 reshape.80
  (7 shorter events, 0.2 us)
Async XLA Ops:
  6.5 54.8 %reduce-scatter.2.cloned.1.call-start = ((), (), s32[]{:S(2)}) async-start(), calls=%async_computation.4 | async-start | bytes 344064 | tf_op jit(solution)/shard_map/reduce_scatter | solution.py:54
Sparse Core Ops, SparseCore 0:
  51.8 9.4 reduce-scatter.1
